TPU v7x, 32 devices: a 4x2x2 block of a 4x4x8 slice. The times are simulated.
32 devices in a mesh: prob: 4 (over y, z), feat: 8 (over x, core).
Axes of the slice: x: 4, y: 2, z: 2, core: 2. Of those that a mesh axis runs over, the one named last changes fastest.
The devices are a block of a 4x4x8 slice.
Arguments:
- design: bfloat16 [65536, 2048], P('prob', 'feat'), parts along dimension 0
- coef_init: float32 [8192, 1], P(('prob', 'feat')), parts along dimension 0
- targets: float32 [65536, 1], P('prob'), parts along dimension 0
- step_sizes: float32 [8192], P(('prob', 'feat')), parts along dimension 0
Outputs:
- output 1: float32 [8192, 1], P(('prob', 'feat')), parts along dimension 0
- output 2: float32 [65536, 1], P('prob'), parts along dimension 0
There are 4 independent parts. A program takes and returns all parts, laid end to end along the dimension named above; each array names one.
All inputs are finite; a program needn't handle non-finite values.
Results may differ from a plain program's by a relative error of at most 0.00472782.
Values are sent between devices in bfloat16 or wider.
A program may use at most 768 MiB of HBM per device.

v0:
```python
import jax
import jax.numpy as jnp
from jax import lax
from jax.sharding import PartitionSpec as P

SWEEPS = 6
COMBINE_WEIGHT = 0.8


def solution(mesh):
    group_size = mesh.shape['feat']

    def local_run(x_local, coef_local, targets_local, step_local):
        samples = x_local.shape[0]
        features = x_local.shape[1] * group_size
        lasso_weight = 0.3 * group_size / features ** 0.5
        step_col = step_local[:, None]
        thresholds = step_col * lasso_weight

        def summed_product(values):
            product = jnp.dot(x_local, values.astype(jnp.bfloat16), preferred_element_type=jnp.float32)
            return lax.psum(product.astype(jnp.bfloat16).astype(jnp.float32), 'feat')

        weights = coef_local
        residual = targets_local - summed_product(weights)
        for _ in range(SWEEPS):
            gradient = lax.dot_general(x_local, residual.astype(jnp.bfloat16), (((0,), (0,)), ((), ())), preferred_element_type=jnp.float32) / samples
            stepped = weights + step_col * gradient
            shrunk = jnp.sign(stepped) * jnp.maximum(jnp.abs(stepped) - thresholds, 0.0)
            change = shrunk - weights
            weights = weights + COMBINE_WEIGHT * change
            residual = residual - COMBINE_WEIGHT * summed_product(change)
        return weights, residual

    return jax.shard_map(local_run, mesh=mesh, in_specs=(P('prob', 'feat'), P(('prob', 'feat'), None), P('prob', None), P(('prob', 'feat'))), out_specs=(P(('prob', 'feat'), None), P('prob', None)), check_vma=False)
```

profile of v0, /device:TPU:81, one launch (start us, length us, event | category | flops | bytes accessed | tf_op | source)
XLA Modules:
  0.0 461.0 jit_solution(18378257952268510803)
XLA Ops:
  7.2 0.0 copy-start.3
  7.2 0.1 all-reduce.8.cloned.1.call-start
  7.3 5.6 %fusion.24 = f32[1,16384]{1,0:T(1,128)S(1)} fusion(bf16[16384,256]{1,0:T(8,128)(2,1)} %param.4, f32[256,1]{0,1:T(1,128)} %param.5), kind=kOutput, calls=%fused_computation.55 | convolution fusion | flops 8388864 | bytes 8455168 | tf_op jit(solution)/shard_map/dot_general | solution.py:21
  12.9 0.7 convert_convert_fusion.6
  13.6 0.1 all-reduce.8.cloned.1.call-update
  13.6 0.1 all-reduce.10.cloned.1.call-start
  13.7 55.5 %all-reduce.8.cloned.1.call-done = f32[16384,1]{0,1:T(1,128)} async-done(((f32[16384,1]{0,1:T(1,128)}), f32[16384,1]{0,1:T(1,128)}) %all-reduce.8.cloned.1.call-update) | async-done | bytes 65552 | tf_op jit(solution)/shard_map/psum | solution.py:22
  69.1 0.9 sub.57
  70.1 4.6 fusion.10
  74.7 5.6 %fusion.22 = f32[1,16384]{1,0:T(1,128)S(1)} fusion(bf16[16384,256]{1,0:T(8,128)(2,1)} %param.4, f32[256,1]{0,1:T(1,128)S(1)} %copy-done.5, f32[256,1]{0,1:T(1,128)S(1)} %bitcast.54, f32[256,1]{0,1:T(1,128)S(1)} %bitcast.69), kind=kOutput, calls=%fused_computation.50 | convolution fusion | flops 8390656 | bytes 8457216 | tf_op jit(solution)/shard_map/dot_general | solution.py:21
  80.3 0.7 convert_convert_fusion.5
  80.9 0.1 all-reduce.10.cloned.1.call-update
  81.0 0.1 all-reduce.12.cloned.1.call-start
  81.1 52.4 %all-reduce.10.cloned.1.call-done = f32[16384,1]{0,1:T(1,128)} async-done(((f32[16384,1]{0,1:T(1,128)}), f32[16384,1]{0,1:T(1,128)}) %all-reduce.10.cloned.1.call-update) | async-done | bytes 65552 | tf_op jit(solution)/shard_map/psum | solution.py:22
  133.5 4.6 %fusion.8 = f32[1,256]{1,0:T(1,128)S(1)} fusion(bf16[16384,256]{1,0:T(8,128)(2,1)} %param.4, f32[16384,1]{0,1:T(1,128)S(1)} %sub.57, f32[16384,1]{0,1:T(1,128)} %all-reduce.10.cloned.1.call-done), kind=kOutput, calls=%fused_computation.13 | convolution fusion | flops 8437760 | bytes 8520704 | tf_op jit(solution)/shard_map/dot_general | solution.py:27
  138.1 5.6 %fusion.20 = f32[1,16384]{1,0:T(1,128)S(1)} fusion(bf16[16384,256]{1,0:T(8,128)(2,1)} %param.4, f32[256,1]{0,1:T(1,128)S(1)} %bitcast.55, f32[256,1]{0,1:T(1,128)S(1)} %bitcast.74, f32[256,1]{0,1:T(1,128)S(1)} %copy-done.5, f32[256,1]{0,1:T(1,128)S(1)} %bitcast.70), kind=kOutput, calls=%fused_computation.45 | convolution fusion | flops 8392960 | bytes 8458240 | tf_op jit(solution)/shard_map/dot_general | solution.py:21
  143.7 0.7 convert_convert_fusion.4
  144.4 0.1 all-reduce.12.cloned.1.call-update
  144.5 0.1 all-reduce.14.cloned.1.call-start
  144.6 52.4 %all-reduce.12.cloned.1.call-done = f32[16384,1]{0,1:T(1,128)} async-done(((f32[16384,1]{0,1:T(1,128)}), f32[16384,1]{0,1:T(1,128)}) %all-reduce.12.cloned.1.call-update) | async-done | bytes 65552 | tf_op jit(solution)/shard_map/psum | solution.py:22
  196.9 1.0 multiply_subtract_fusion.4
  197.9 4.6 fusion.6
  202.5 5.6 %fusion.18 = f32[1,16384]{1,0:T(1,128)S(1)} fusion(bf16[16384,256]{1,0:T(8,128)(2,1)} %param.4, f32[256,1]{0,1:T(1,128)S(1)} %multiply_add_fusion.4, f32[256,1]{0,1:T(1,128)S(1)} %bitcast.57, f32[256,1]{0,1:T(1,128)S(1)} %bitcast.63), kind=kOutput, calls=%fused_computation.40 | convolution fusion | flops 8390656 | bytes 8457216 | tf_op jit(solution)/shard_map/dot_general | solution.py:21
  208.1 0.7 convert_convert_fusion.3
  208.8 0.1 all-reduce.14.cloned.1.call-update
  208.8 0.1 all-reduce.16.cloned.1.call-start
  208.9 52.4 %all-reduce.14.cloned.1.call-done = f32[16384,1]{0,1:T(1,128)} async-done(((f32[16384,1]{0,1:T(1,128)}), f32[16384,1]{0,1:T(1,128)}) %all-reduce.14.cloned.1.call-update) | async-done | bytes 65552 | tf_op jit(solution)/shard_map/psum | solution.py:22
  261.3 4.6 %fusion.4 = f32[1,256]{1,0:T(1,128)S(1)} fusion(bf16[16384,256]{1,0:T(8,128)(2,1)} %param.4, f32[16384,1]{0,1:T(1,128)S(1)} %multiply_subtract_fusion.4, f32[16384,1]{0,1:T(1,128)} %all-reduce.14.cloned.1.call-done), kind=kOutput, calls=%fused_computation.7 | convolution fusion | flops 8437760 | bytes 8520704 | tf_op jit(solution)/shard_map/dot_general | solution.py:27
  265.9 5.6 %fusion.16 = f32[1,16384]{1,0:T(1,128)S(1)} fusion(bf16[16384,256]{1,0:T(8,128)(2,1)} %param.4, f32[256,1]{0,1:T(1,128)S(1)} %bitcast.58, f32[256,1]{0,1:T(1,128)S(1)} %bitcast.72, f32[256,1]{0,1:T(1,128)S(1)} %multiply_add_fusion.4, f32[256,1]{0,1:T(1,128)S(1)} %bitcast.64), kind=kOutput, calls=%fused_computation.35 | convolution fusion | flops 8392960 | bytes 8458240 | tf_op jit(solution)/shard_map/dot_general | solution.py:21
  271.6 0.7 convert_convert_fusion.2
  272.2 0.1 all-reduce.16.cloned.1.call-update
  272.3 0.2 all-reduce.18.cloned.1.call-start
  272.6 52.2 %all-reduce.16.cloned.1.call-done = f32[16384,1]{0,1:T(1,128)} async-done(((f32[16384,1]{0,1:T(1,128)}), f32[16384,1]{0,1:T(1,128)}) %all-reduce.16.cloned.1.call-update) | async-done | bytes 65552 | tf_op jit(solution)/shard_map/psum | solution.py:22
  324.7 0.0 copy-done
  324.7 1.0 multiply_subtract_fusion.2
  325.7 4.6 fusion.2
  330.3 5.6 %fusion.14 = f32[1,16384]{1,0:T(1,128)S(1)} fusion(bf16[16384,256]{1,0:T(8,128)(2,1)} %param.4, f32[256,1]{0,1:T(1,128)S(1)} %multiply_add_fusion.2, f32[256,1]{0,1:T(1,128)S(1)} %bitcast.60, f32[256,1]{0,1:T(1,128)S(1)} %bitcast.66), kind=kOutput, calls=%fused_computation.30 | convolution fusion | flops 8390656 | bytes 8457216 | tf_op jit(solution)/shard_map/dot_general | solution.py:21
  335.9 0.7 convert_convert_fusion.1
  336.6 0.1 all-reduce.18.cloned.1.call-update
  336.7 0.1 all-reduce.20.cloned.1.call-start
  336.7 52.4 %all-reduce.18.cloned.1.call-done = f32[16384,1]{0,1:T(1,128)} async-done(((f32[16384,1]{0,1:T(1,128)}), f32[16384,1]{0,1:T(1,128)}) %all-reduce.18.cloned.1.call-update) | async-done | bytes 65552 | tf_op jit(solution)/shard_map/psum | solution.py:22
  389.1 4.6 %fusion = f32[1,256]{1,0:T(1,128)S(1)} fusion(bf16[16384,256]{1,0:T(8,128)(2,1)} %param.4, f32[16384,1]{0,1:T(1,128)S(1)} %multiply_subtract_fusion.2, f32[16384,1]{0,1:T(1,128)} %all-reduce.18.cloned.1.call-done), kind=kOutput, calls=%fused_computation.1 | convolution fusion | flops 8437760 | bytes 8520704 | tf_op jit(solution)/shard_map/dot_general | solution.py:27
  393.8 5.6 %fusion.12 = f32[1,16384]{1,0:T(1,128)S(1)} fusion(bf16[16384,256]{1,0:T(8,128)(2,1)} %param.4, f32[256,1]{0,1:T(1,128)S(1)} %bitcast.61, f32[256,1]{0,1:T(1,128)S(1)} %bitcast.76, f32[256,1]{0,1:T(1,128)S(1)} %multiply_add_fusion.2, f32[256,1]{0,1:T(1,128)S(1)} %bitcast.67), kind=kOutput, calls=%fused_computation.25 | convolution fusion | flops 8392960 | bytes 8458240 | tf_op jit(solution)/shard_map/dot_general | solution.py:21
  399.4 0.7 convert_convert_fusion
  400.0 0.1 all-reduce.20.cloned.1.call-update
  400.1 0.6 multiply_add_fusion
  400.7 51.9 %all-reduce.20.cloned.1.call-done = f32[16384,1]{0,1:T(1,128)} async-done(((f32[16384,1]{0,1:T(1,128)}), f32[16384,1]{0,1:T(1,128)}) %all-reduce.20.cloned.1.call-update) | async-done | bytes 65552 | tf_op jit(solution)/shard_map/psum | solution.py:22
  452.6 1.6 multiply_subtract_fusion
  (18 shorter events, 0.1 us)
Async XLA Ops:
  7.2 62.0 %copy-start.3 = (f32[16384,1]{0,1:T(1,128)S(1)}, f32[16384,1]{0,1:T(1,128)}, u32[]{:S(2)}) copy-start(f32[16384,1]{0,1:T(1,128)} %param.6) | copy-start | bytes 196612
  7.2 62.0 %all-reduce.8.cloned.1.call-start = ((), (), s32[]{:S(2)}) async-start(), calls=%async_computation | async-start | bytes 131072 | tf_op jit(solution)/shard_map/psum | solution.py:22
  12.9 61.7 %copy-start.4 = (f32[256]{0:T(256)S(1)}, f32[256]{0:T(256)}, u32[]{:S(2)}) copy-start(f32[256]{0:T(256)} %param.7) | copy-start | bytes 3076
  12.9 61.8 %copy-start.5 = (f32[256,1]{0,1:T(1,128)S(1)}, f32[256,1]{0,1:T(1,128)}, u32[]{:S(2)}) copy-start(f32[256,1]{0,1:T(1,128)} %param.5) | copy-start | bytes 3076
  13.6 119.8 %all-reduce.10.cloned.1.call-start = ((), (), s32[]{:S(2)}) async-start(), calls=%async_computation.1 | async-start | bytes 131072 | tf_op jit(solution)/shard_map/psum | solution.py:22
  81.0 115.9 %all-reduce.12.cloned.1.call-start = ((), (), s32[]{:S(2)}) async-start(), calls=%async_computation.2 | async-start | bytes 131072 | tf_op jit(solution)/shard_map/psum | solution.py:22
  133.5 63.5 %copy-start.1 = (f32[16384,1]{0,1:T(1,128)S(1)}, f32[16384,1]{0,1:T(1,128)}, u32[]{:S(2)}) copy-start(f32[16384,1]{0,1:T(1,128)} %all-reduce.10.cloned.1.call-done) | copy-start | bytes 196612
  144.5 116.8 %all-reduce.14.cloned.1.call-start = ((), (), s32[]{:S(2)}) async-start(), calls=%async_computation.3 | async-start | bytes 131072 | tf_op jit(solution)/shard_map/psum | solution.py:22
  208.8 115.9 %all-reduce.16.cloned.1.call-start = ((), (), s32[]{:S(2)}) async-start(), calls=%async_computation.4 | async-start | bytes 131072 | tf_op jit(solution)/shard_map/psum | solution.py:22
  261.3 63.5 %copy-start = (f32[16384,1]{0,1:T(1,128)S(1)}, f32[16384,1]{0,1:T(1,128)}, u32[]{:S(2)}) copy-start(f32[16384,1]{0,1:T(1,128)} %all-reduce.14.cloned.1.call-done) | copy-start | bytes 196612
  272.3 116.8 %all-reduce.18.cloned.1.call-start = ((), (), s32[]{:S(2)}) async-start(), calls=%async_computation.5 | async-start | bytes 131072 | tf_op jit(solution)/shard_map/psum | solution.py:22
  336.7 115.9 %all-reduce.20.cloned.1.call-start = ((), (), s32[]{:S(2)}) async-start(), calls=%async_computation.6 | async-start | bytes 131072 | tf_op jit(solution)/shard_map/psum | solution.py:22
  389.1 63.5 %copy-start.2 = (f32[16384,1]{0,1:T(1,128)S(1)}, f32[16384,1]{0,1:T(1,128)}, u32[]{:S(2)}) copy-start(f32[16384,1]{0,1:T(1,128)} %all-reduce.18.cloned.1.call-done) | copy-start | bytes 196612
Sparse Core Ops, SparseCore 0:
  13.7 55.3 all-reduce.7
  81.1 52.2 all-reduce.9
  144.6 52.2 all-reduce.11
  208.9 52.2 all-reduce.13
  272.4 52.2 all-reduce.15
  336.8 52.2 all-reduce.17
  400.2 52.2 all-reduce.19
where the time goes:
time: 463 us; the launch traced here: 461 us
  waiting for transfers between devices  369 us (80%)
  matrix products  67.1 us (14%)
  between operations  14.2 us (3%)
  other arithmetic  9.7 us (2%)
    psum x7, waiting for transfers between devices, summed_product(): return lax.psum(product.astype(jnp.bfloat16).astype(jnp.float32), 'feat')  369 us
    dot_general x7, matrix products, summed_product(): jnp.dot(x_local, values.astype(jnp.bfloat16), preferred_element_type=jnp....  39.5 us
    dot_general x6, matrix products, local_run(): lax.dot_general(x_local, residual.astype(jnp.bfloat16), (((0,), (0,)), ((...  27.6 us
  transfers between devices with their start and end apart: 7, of which 7 were waited for; matrix products, arithmetic and copies ran while one was open for 0% of the time, Pallas kernels for 0%

commit v1 on v0

v1 whole, which is shorter than its diff:
```python
import functools

import jax
import jax.numpy as jnp
from jax import lax
from jax.experimental import pallas as pl
from jax.experimental.pallas import tpu as pltpu
from jax.sharding import PartitionSpec as P

SWEEPS = 6
COMBINE_WEIGHT = 0.8
MESH = pl.DeviceIdType.MESH
LANES = 128
ROWS = 16
CHUNK = 2 * ROWS * LANES
LOADS = 8


def kernel(size, lasso_weight, x_hbm, w_ref, y_ref, eta_ref, w_out, r_out, xv, xt, ubuf, rbf, res, dmat, wcur, load_sem, send_sem, recv_sem, rsend_sem, rrecv_sem):
    samples, feats = x_hbm.shape
    chunks = samples // CHUNK
    qrows = CHUNK // LANES
    chips = size // 2
    me = lax.axis_index('feat')
    chip, core = me // 2, lax.rem(me, 2)
    sibling = 2 * chip + 1 - core
    lead = core == 1

    load_rows = samples // LOADS
    loads = [pltpu.make_async_copy(x_hbm.at[pl.ds(i * load_rows, load_rows)], xv.at[pl.ds(i * load_rows, load_rows)], load_sem.at[i]) for i in range(LOADS)]
    for load in loads:
        load.start()

    barrier = pltpu.get_barrier_semaphore()
    for d in range(1, size):
        pl.semaphore_signal(barrier, inc=1, device_id={'feat': lax.rem(me + d, size)}, device_id_type=MESH)

    row_id = lax.broadcasted_iota(jnp.int32, (ROWS, LANES), 0)

    def set_dmat(values):
        for h in range(feats // LANES):
            piece = jnp.broadcast_to(values[:, h * LANES:(h + 1) * LANES], (ROWS, LANES))
            for m in range(ROWS):
                dmat[:, m * feats + h * LANES:m * feats + (h + 1) * LANES] = jnp.where(row_id == m, piece, 0.0).astype(jnp.bfloat16)

    def u_copy(par, g, dest, slot):
        here = ubuf.at[par, me, pl.ds(g * qrows, qrows)]
        return pltpu.make_async_remote_copy(src_ref=here, dst_ref=here, send_sem=send_sem.at[g, slot], recv_sem=recv_sem.at[par, g, me], device_id={'feat': dest}, device_id_type=MESH)

    far_order = [chips // 2] + [d for d in range(1, chips) if d != chips // 2]

    def u_chunk(par, g):
        u = jnp.dot(dmat[...], xt[pl.ds(g * CHUNK, CHUNK), :], preferred_element_type=jnp.float32).astype(jnp.bfloat16)
        ubuf[par, me, pl.ds(g * qrows, ROWS), :] = u[:, :LANES]
        ubuf[par, me, pl.ds(g * qrows + ROWS, ROWS), :] = u[:, LANES:]
        for slot, d in enumerate(far_order):
            u_copy(par, g, 2 * lax.rem(chip + d, chips) + 1, slot).start()

        @pl.when(core == 0)
        def _():
            u_copy(par, g, sibling, chips - 1).start()

    def u_wait_sends(par):
        for g in range(chunks):
            for slot in range(chips - 1):
                u_copy(par, g, sibling, slot).wait_send()

            @pl.when(core == 0)
            def _():
                u_copy(par, g, sibling, chips - 1).wait_send()

    def r_copy(buf, g):
        here = buf.at[pl.ds(g * qrows, qrows)]
        return pltpu.make_async_remote_copy(src_ref=here, dst_ref=here, send_sem=rsend_sem.at[g], recv_sem=rrecv_sem.at[g], device_id={'feat': sibling}, device_id_type=MESH)

    def new_residual(par, g, factor):
        for d in range(1, size):
            src = lax.rem(me + d, size)
            there = ubuf.at[par, src, pl.ds(g * qrows, qrows)]
            pltpu.make_async_remote_copy(src_ref=there, dst_ref=there, send_sem=send_sem.at[g, 0], recv_sem=recv_sem.at[par, g, src], device_id={'feat': src}, device_id_type=MESH).wait_recv()
        total = ubuf[par, 0, pl.ds(g * qrows, qrows), :].astype(jnp.float32)
        for s in range(1, size):
            total = total + ubuf[par, s, pl.ds(g * qrows, qrows), :].astype(jnp.float32)
        return res[pl.ds(g * qrows, qrows), :] - factor * total

    res[...] = y_ref[...]
    wcur[...] = w_ref[...]
    set_dmat(w_ref[...])

    per_chunk = LOADS // chunks
    for g in range(chunks):
        for i in range(per_chunk):
            loads[g * per_chunk + i].wait()

        @pl.loop(0, ROWS)
        def _(m):
            for h in range(2):
                src = pl.multiple_of(g * CHUNK + h * ROWS * LANES + m * LANES, LANES)
                dst = pl.multiple_of(g * CHUNK + m * feats, feats)
                xt[pl.ds(dst, feats), h * LANES:(h + 1) * LANES] = xv[pl.ds(src, LANES), :].T

    pl.semaphore_wait(barrier, size - 1)

    @pl.loop(0, SWEEPS)
    def _(t):
        par = lax.rem(t, 2)
        factor = jnp.where(t == 0, 1.0, COMBINE_WEIGHT).astype(jnp.float32)
        for g in range(chunks):
            u_chunk(par, g)

        grad = jnp.zeros((ROWS, feats), jnp.float32)
        for g in range(chunks):
            @pl.when(lead)
            def _():
                r = new_residual(par, g, factor)
                res[pl.ds(g * qrows, qrows), :] = r
                rbf[pl.ds(g * qrows, qrows), :] = r.astype(jnp.bfloat16)
                r_copy(rbf, g).start()

            @pl.when(core == 0)
            def _():
                r_copy(rbf, g).wait_recv()

            zero = jnp.zeros((ROWS, LANES), jnp.float32)
            halves = [rbf[pl.ds(g * qrows + h * ROWS, ROWS), :].astype(jnp.float32) for h in range(2)]
            left = jnp.concatenate([jnp.where(row_id == m, halves[h], zero).astype(jnp.bfloat16) for h in range(2) for m in range(ROWS)], axis=1)
            grad = grad + jnp.dot(left, xv[pl.ds(g * CHUNK, CHUNK), :], preferred_element_type=jnp.float32)

        gradient = jnp.sum(grad, axis=0, keepdims=True) * (1.0 / samples)
        weights = wcur[...]
        eta = eta_ref[...]
        threshold = eta * lasso_weight
        stepped = weights + eta * gradient
        shrunk = jnp.maximum(stepped - threshold, 0.0) + jnp.minimum(stepped + threshold, 0.0)
        change = shrunk - weights
        wcur[...] = weights + COMBINE_WEIGHT * change
        set_dmat(change)
        u_wait_sends(par)

        @pl.when(lead)
        def _():
            for g in range(chunks):
                r_copy(rbf, g).wait_send()

    last = SWEEPS % 2
    for g in range(chunks):
        u_chunk(last, g)
    w_out[...] = wcur[...]
    for g in range(chunks):
        @pl.when(lead)
        def _():
            res[pl.ds(g * qrows, qrows), :] = new_residual(last, g, COMBINE_WEIGHT)
            r_copy(res, g).start()
    for g in range(chunks):
        @pl.when(core == 0)
        def _():
            r_copy(res, g).wait_recv()
    r_out[...] = res[...]
    u_wait_sends(last)

    @pl.when(lead)
    def _():
        for g in range(chunks):
            r_copy(res, g).wait_send()


def solution(mesh):
    size = mesh.shape['feat']

    def local_run(x_local, coef_local, targets_local, step_local):
        samples, feats = x_local.shape
        chunks = samples // CHUNK
        lasso_weight = 0.3 * size / (feats * size) ** 0.5
        vmem = pl.BlockSpec(memory_space=pltpu.VMEM)
        weights, residual = pl.pallas_call(
            functools.partial(kernel, size, lasso_weight),
            out_shape=(jax.ShapeDtypeStruct((1, feats), jnp.float32), jax.ShapeDtypeStruct((samples // LANES, LANES), jnp.float32)),
            in_specs=[pl.BlockSpec(memory_space=pl.ANY), vmem, vmem, vmem],
            out_specs=(vmem, vmem),
            scratch_shapes=[
                pltpu.VMEM((samples, feats), jnp.bfloat16),
                pltpu.VMEM((samples, feats), jnp.bfloat16),
                pltpu.VMEM((2, size, samples // LANES, LANES), jnp.bfloat16),
                pltpu.VMEM((samples // LANES, LANES), jnp.bfloat16),
                pltpu.VMEM((samples // LANES, LANES), jnp.float32),
                pltpu.VMEM((ROWS, ROWS * feats), jnp.bfloat16),
                pltpu.VMEM((1, feats), jnp.float32),
                pltpu.SemaphoreType.DMA((LOADS,)),
                pltpu.SemaphoreType.DMA((chunks, size // 2)),
                pltpu.SemaphoreType.DMA((2, chunks, size)),
                pltpu.SemaphoreType.DMA((chunks,)),
                pltpu.SemaphoreType.DMA((chunks,)),
            ],
            compiler_params=pltpu.CompilerParams(collective_id=0, has_side_effects=True),
        )(x_local, coef_local.reshape(1, feats), targets_local.reshape(samples // LANES, LANES), step_local.reshape(1, feats))
        return weights.reshape(feats, 1), residual.reshape(samples, 1)

    return jax.shard_map(local_run, mesh=mesh, in_specs=(P('prob', 'feat'), P(('prob', 'feat'), None), P('prob', None), P(('prob', 'feat'))), out_specs=(P(('prob', 'feat'), None), P('prob', None)), check_vma=False)
```

time: 463 us -> 68.1 us (0.15)
  waiting for transfers between devices: 369 us -> 0 us
  matrix products: 67.1 us -> 0 us
  Pallas kernels: 0 us -> 64.6 us
  between operations: 14.2 us -> 0.64 us
  other arithmetic: 9.7 us -> 0 us
    psum x7 -> x0, waiting for transfers between devices: 369 us -> none  [summed_product(): return lax.psum(product.astype(jnp.bfloat16).astype(jnp.float32), 'feat')]
    dot_general x13 -> x0, matrix products: 67.1 us -> none  [the longest x7 39.5 us: summed_product(): jnp.dot(x_local, values.astype(jnp.bfloat16), preferred_element_type=jnp....]
    pallas_call x0 -> x1, Pallas kernels: none -> 64.6 us  [local_run(): pl.pallas_call(functools.partial(kernel, size, lasso_weight), out_shape=(...]
  transfers between devices with their start and end apart: 7 -> 0, of which waited for: 7 -> 0; matrix products, arithmetic and copies ran while one was open for 0% -> 0% of each run, Pallas kernels for 0% -> 0%
where the time goes in v1:
time: 68.1 us; the launch traced here: 67.9 us
  Pallas kernels  64.6 us (95%)
  local copies, waits for them, and re-layouts  2.67 us (4%)
    pallas_call x1, Pallas kernels, local_run(): pl.pallas_call(functools.partial(kernel, size, lasso_weight), out_shape=(...  64.6 us
    unnamed x2, local copies, waits for them, and re-layouts  2.67 us

profile of v1, /device:TPU:81, one launch (start us, length us, event | category | flops | bytes accessed | tf_op | source)
XLA Modules:
  0.0 67.9 jit_solution(208381841329028748)
XLA Ops:
  0.6 64.6 %shard_map.59 = (f32[1,256]{1,0:T(1,128)}, f32[128,128]{1,0:T(8,128)}) custom-call(bf16[16384,256]{1,0:T(8,128)(2,1)} %x_hbm.1, f32[1,256]{1,0:T(1,128)} %bitcast.7, f32[128,128]{1,0:T(8,128)} %bitcast.5, f32[1,256]{1,0:T(1,128)} %bitcast.8), custom_call_target="tpu_custom_call" | custom-call | tf_op jit(solution)/shard_map/pallas_call | solution.py:175
  65.3 1.2 %copy.8 = f32[256,1]{0,1:T(1,128)} copy(f32[256,1]{0,1:T(1,128)} %bitcast.9) | data formatting | bytes 2048
  66.5 1.5 %copy.9 = f32[16384,1]{0,1:T(1,128)} copy(f32[16384,1]{0,1:T(1,128)} %bitcast.6) | data formatting | bytes 131072

commit v2 on v1

v2 whole, which is shorter than its diff:
```python
import functools

import jax
import jax.numpy as jnp
from jax import lax
from jax.experimental import pallas as pl
from jax.experimental.pallas import tpu as pltpu
from jax.sharding import PartitionSpec as P

SWEEPS = 6
COMBINE_WEIGHT = 0.8
MESH = pl.DeviceIdType.MESH
LANES = 128
SUB = 8
TILE = 2 * LANES
UNIT = SUB * TILE
CHUNK = 2 * UNIT


def kernel(size, lasso_weight, x_hbm, w_ref, y_ref, eta_ref, w_out, r_out, xv, xt, ubuf, rbf, res, dmat, wcur, load_sem, send_sem, recv_sem, rsend_sem, rrecv_sem):
    samples = x_hbm.shape[0]
    chunks = samples // CHUNK
    qrows = CHUNK // LANES
    chips = size // 2
    me = lax.axis_index('feat')
    chip, core = me // 2, lax.rem(me, 2)
    sibling = 2 * chip + 1 - core
    lead = core == 1
    far_order = [chips // 2] + [d for d in range(1, chips) if d != chips // 2]

    loads = [pltpu.make_async_copy(x_hbm.at[pl.ds(g * CHUNK, CHUNK)], xv.at[pl.ds(g * CHUNK, CHUNK)], load_sem.at[g]) for g in range(chunks)]
    for load in loads:
        load.start()

    barrier = pltpu.get_barrier_semaphore()
    for d in range(1, size):
        pl.semaphore_signal(barrier, inc=1, device_id={'feat': lax.rem(me + d, size)}, device_id_type=MESH)

    row_id = lax.broadcasted_iota(jnp.int32, (SUB, TILE), 0)

    def set_dmat(values):
        spread = jnp.broadcast_to(values, (SUB, TILE))
        for m in range(SUB):
            dmat[:, m * TILE:(m + 1) * TILE] = jnp.where(row_id == m, spread, 0.0).astype(jnp.bfloat16)

    def u_copy(par, g, dest, slot):
        here = ubuf.at[par, me, pl.ds(g * qrows, qrows)]
        return pltpu.make_async_remote_copy(src_ref=here, dst_ref=here, send_sem=send_sem.at[par, g, slot], recv_sem=recv_sem.at[par, g, me], device_id={'feat': dest}, device_id_type=MESH)

    def u_half(g, part):
        out = []
        for q in range(2):
            base = (2 * g + q) * UNIT + part * UNIT // 2
            left = dmat[:, part * UNIT // 2:(part + 1) * UNIT // 2]
            out.append(jnp.dot(left, xt[pl.ds(base, UNIT // 2), :], preferred_element_type=jnp.float32))
        return out

    def u_first(g, part):
        out = []
        for q in range(2):
            base = (2 * g + q) * UNIT
            left = dmat[:, part * UNIT // 2:(part + 1) * UNIT // 2]
            rhs = jnp.concatenate([jnp.concatenate([xv[pl.ds(base + (h * SUB + m) * LANES, LANES), :] for h in range(2)], axis=0) for m in range(part * SUB // 2, (part + 1) * SUB // 2)], axis=1)
            out.append(lax.dot_general(left, rhs, (((1,), (1,)), ((), ())), preferred_element_type=jnp.float32))
        return out

    def u_finish(par, g, halves):
        for q in range(2):
            u = halves[0][q] + halves[1][q]
            u = jnp.concatenate([u[:, :LANES], u[:, LANES:]], axis=0).astype(jnp.bfloat16)
            ubuf[par, me, pl.ds(g * qrows + q * 2 * SUB, 2 * SUB), :] = u
        for slot, d in enumerate(far_order):
            u_copy(par, g, 2 * lax.rem(chip + d, chips) + 1, slot).start()

        @pl.when(core == 0)
        def _():
            u_copy(par, g, sibling, chips - 1).start()

    def products(par):
        start = u_half(0, 0)
        for g in range(chunks):
            end = u_half(g, 1)
            following = u_half(g + 1, 0) if g + 1 < chunks else None
            u_finish(par, g, (start, end))
            start = following

    def u_wait_sends(par):
        for g in range(chunks):
            for slot in range(chips - 1):
                u_copy(par, g, sibling, slot).wait_send()

            @pl.when(core == 0)
            def _():
                u_copy(par, g, sibling, chips - 1).wait_send()

    def r_copy(buf, g):
        here = buf.at[pl.ds(g * qrows, qrows)]
        return pltpu.make_async_remote_copy(src_ref=here, dst_ref=here, send_sem=rsend_sem.at[g], recv_sem=rrecv_sem.at[g], device_id={'feat': sibling}, device_id_type=MESH)

    def new_residual(par, g, factor):
        for d in range(1, size):
            src = lax.rem(me + d, size)
            there = ubuf.at[par, src, pl.ds(g * qrows, qrows)]
            pltpu.make_async_remote_copy(src_ref=there, dst_ref=there, send_sem=send_sem.at[par, g, 0], recv_sem=recv_sem.at[par, g, src], device_id={'feat': src}, device_id_type=MESH).wait_recv()
        total = ubuf[par, 0, pl.ds(g * qrows, qrows), :].astype(jnp.float32)
        for s in range(1, size):
            total = total + ubuf[par, s, pl.ds(g * qrows, qrows), :].astype(jnp.float32)
        return res[pl.ds(g * qrows, qrows), :] - factor * total

    def residual_and_gradient(par, factor):
        grads = [jnp.zeros((SUB, TILE), jnp.float32)] * 2
        for g in range(chunks):
            @pl.when(lead)
            def _():
                r = new_residual(par, g, factor)
                res[pl.ds(g * qrows, qrows), :] = r
                rbf[pl.ds(g * qrows, qrows), :] = r.astype(jnp.bfloat16)
                r_copy(rbf, g).start()

            @pl.when(core == 0)
            def _():
                r_copy(rbf, g).wait_recv()

            r = rbf[pl.ds(g * qrows, qrows), :].astype(jnp.float32)
            for q in range(2):
                pieces = []
                for k in range(2 * SUB):
                    base = q * 2 * SUB + k // SUB * SUB
                    pieces.append(jnp.where(row_id[:, :LANES] == k % SUB, r[base:base + SUB], 0.0).astype(jnp.bfloat16))
                left = jnp.concatenate(pieces, axis=1)
                grads[q] = grads[q] + jnp.dot(left, xv[pl.ds((2 * g + q) * UNIT, UNIT), :], preferred_element_type=jnp.float32)
        total = jnp.sum(grads[0], axis=0, keepdims=True) + jnp.sum(grads[1], axis=0, keepdims=True)
        return total * (1.0 / samples)

    def update(gradient):
        weights = wcur[...]
        eta = eta_ref[...]
        threshold = eta * lasso_weight
        stepped = weights + eta * gradient
        shrunk = jnp.maximum(stepped - threshold, 0.0) + jnp.minimum(stepped + threshold, 0.0)
        change = shrunk - weights
        wcur[...] = weights + COMBINE_WEIGHT * change
        set_dmat(change)

    def sweep_end(par):
        u_wait_sends(par)

        @pl.when(lead)
        def _():
            for g in range(chunks):
                r_copy(rbf, g).wait_send()

    res[...] = y_ref[...]
    wcur[...] = w_ref[...]
    set_dmat(w_ref[...])

    for g in range(chunks):
        loads[g].wait()
        halves = [u_first(g, part) for part in range(2)]
        if g == 0:
            pl.semaphore_wait(barrier, size - 1)
        u_finish(0, g, halves)

    @pl.loop(0, samples // UNIT)
    def _(unit):
        for m in range(SUB):
            for h in range(2):
                src = pl.multiple_of(unit * UNIT + h * SUB * LANES + m * LANES, LANES)
                dst = pl.multiple_of(unit * UNIT + m * TILE, TILE)
                xt[pl.ds(dst, TILE), h * LANES:(h + 1) * LANES] = xv[pl.ds(src, LANES), :].T

    @pl.loop(0, SWEEPS)
    def _(t):
        par = lax.rem(t, 2)
        factor = jnp.where(t == 0, 1.0, COMBINE_WEIGHT).astype(jnp.float32)
        update(residual_and_gradient(par, factor))
        products(1 - par)
        sweep_end(par)

    last = SWEEPS % 2
    w_out[...] = wcur[...]
    for g in range(chunks):
        @pl.when(lead)
        def _():
            res[pl.ds(g * qrows, qrows), :] = new_residual(last, g, COMBINE_WEIGHT)
            r_copy(res, g).start()
    for g in range(chunks):
        @pl.when(core == 0)
        def _():
            r_copy(res, g).wait_recv()
    r_out[...] = res[...]
    u_wait_sends(last)

    @pl.when(lead)
    def _():
        for g in range(chunks):
            r_copy(res, g).wait_send()


def solution(mesh):
    size = mesh.shape['feat']

    def local_run(x_local, coef_local, targets_local, step_local):
        samples, feats = x_local.shape
        chunks = samples // CHUNK
        lasso_weight = 0.3 * size / (feats * size) ** 0.5
        vmem = pl.BlockSpec(memory_space=pltpu.VMEM)
        weights, residual = pl.pallas_call(
            functools.partial(kernel, size, lasso_weight),
            out_shape=(jax.ShapeDtypeStruct((1, feats), jnp.float32), jax.ShapeDtypeStruct((samples // LANES, LANES), jnp.float32)),
            in_specs=[pl.BlockSpec(memory_space=pl.ANY), vmem, vmem, vmem],
            out_specs=(vmem, vmem),
            scratch_shapes=[
                pltpu.VMEM((samples, feats), jnp.bfloat16),
                pltpu.VMEM((samples, feats), jnp.bfloat16),
                pltpu.VMEM((2, size, samples // LANES, LANES), jnp.bfloat16),
                pltpu.VMEM((samples // LANES, LANES), jnp.bfloat16),
                pltpu.VMEM((samples // LANES, LANES), jnp.float32),
                pltpu.VMEM((SUB, SUB * feats), jnp.bfloat16),
                pltpu.VMEM((1, feats), jnp.float32),
                pltpu.SemaphoreType.DMA((chunks,)),
                pltpu.SemaphoreType.DMA((2, chunks, size // 2)),
                pltpu.SemaphoreType.DMA((2, chunks, size)),
                pltpu.SemaphoreType.DMA((chunks,)),
                pltpu.SemaphoreType.DMA((chunks,)),
            ],
            compiler_params=pltpu.CompilerParams(collective_id=0, has_side_effects=True),
        )(x_local, coef_local.reshape(1, feats), targets_local.reshape(samples // LANES, LANES), step_local.reshape(1, feats))
        return weights.reshape(feats, 1), residual.reshape(samples, 1)

    return jax.shard_map(local_run, mesh=mesh, in_specs=(P('prob', 'feat'), P(('prob', 'feat'), None), P('prob', None), P(('prob', 'feat'))), out_specs=(P(('prob', 'feat'), None), P('prob', None)), check_vma=False)
```

time: 68.1 us -> 53.4 us (0.78)
  Pallas kernels: 64.6 us -> 49.9 us
    pallas_call x1, Pallas kernels: 64.6 us -> 49.9 us  [local_run(): pl.pallas_call(functools.partial(kernel, size, lasso_weight), out_shape=(...]
where the time goes in v2:
time: 53.4 us; the launch traced here: 53.2 us
  Pallas kernels  49.9 us (93%)
  local copies, waits for them, and re-layouts  2.67 us (5%)
  between operations  0.64 us (1%)
    pallas_call x1, Pallas kernels, local_run(): pl.pallas_call(functools.partial(kernel, size, lasso_weight), out_shape=(...  49.9 us
    unnamed x2, local copies, waits for them, and re-layouts  2.67 us

profile of v2, /device:TPU:81, one launch (start us, length us, event | category | flops | bytes accessed | tf_op | source)
XLA Modules:
  0.0 53.2 jit_solution(8797070632521560217)
XLA Ops:
  0.6 49.9 %shard_map.59 = (f32[1,256]{1,0:T(1,128)}, f32[128,128]{1,0:T(8,128)}) custom-call(bf16[16384,256]{1,0:T(8,128)(2,1)} %x_hbm.1, f32[1,256]{1,0:T(1,128)} %bitcast.7, f32[128,128]{1,0:T(8,128)} %bitcast.5, f32[1,256]{1,0:T(1,128)} %bitcast.8), custom_call_target="tpu_custom_call" | custom-call | tf_op jit(solution)/shard_map/pallas_call | solution.py:208
  50.5 1.2 %copy.8 = f32[256,1]{0,1:T(1,128)} copy(f32[256,1]{0,1:T(1,128)} %bitcast.9) | data formatting | bytes 2048
  51.7 1.5 %copy.9 = f32[16384,1]{0,1:T(1,128)} copy(f32[16384,1]{0,1:T(1,128)} %bitcast.6) | data formatting | bytes 131072

commit v3 on v0

v3 whole, which is shorter than its diff:
```python
import functools

import jax
import jax.numpy as jnp
from jax import lax
from jax.experimental import pallas as pl
from jax.experimental.pallas import tpu as pltpu
from jax.sharding import PartitionSpec as P

SWEEPS = 6
COMBINE_WEIGHT = 0.8
MESH = pl.DeviceIdType.MESH
LANES = 128
SUB = 8
ROWS = 16
TILE = 2 * LANES
BLOCK = ROWS * TILE
QROWS = BLOCK // LANES
MATMUL_ROWS = 10
SECTIONS = ((0, 2), (2, 4))


def kernel(size, lasso_weight, x_hbm, w_hbm, y_hbm, eta_hbm, w_out, r_out, xv, xt, ubuf, rbf, res, dmat, dcol, gref, wcur, eta_v, load_sem, small_sem, send_sem, recv_sem, rsend_sem, rrecv_sem):
    samples = x_hbm.shape[0]
    blocks = samples // BLOCK
    chips = size // 2
    me = lax.axis_index('feat')
    chip, core = me // 2, lax.rem(me, 2)
    sibling = 2 * chip + 1 - core
    lead = core == 1
    far_order = [chips // 2] + [d for d in range(1, chips) if d != chips // 2]

    small = [pltpu.make_async_copy(src, dst, small_sem.at[i]) for i, (src, dst) in enumerate(((w_hbm, wcur), (eta_hbm, eta_v), (y_hbm, res)))]
    loads = [pltpu.make_async_copy(x_hbm.at[pl.ds(b * BLOCK, BLOCK)], xv.at[pl.ds(b * BLOCK, BLOCK)], load_sem.at[b]) for b in range(blocks)]
    small[0].start()
    for load in loads:
        load.start()
    for load in small[1:]:
        load.start()

    barrier = pltpu.get_barrier_semaphore()
    for d in range(1, size):
        pl.semaphore_signal(barrier, inc=1, device_id={'feat': lax.rem(me + d, size)}, device_id_type=MESH)

    row16 = lax.broadcasted_iota(jnp.int32, (ROWS, LANES), 0)
    row8 = lax.broadcasted_iota(jnp.int32, (SUB, LANES), 0)

    def set_left(values, rows):
        for h in range(2):
            spread = jnp.broadcast_to(values[:, h * LANES:(h + 1) * LANES], (ROWS, LANES))
            for m in range(rows):
                dmat[:, m * TILE + h * LANES:m * TILE + (h + 1) * LANES] = jnp.where(row16 == m, spread, 0.0).astype(jnp.bfloat16)

    def set_column(values):
        rounded = values.astype(jnp.bfloat16).astype(jnp.float32)
        for h in range(2):
            dcol[h * LANES:(h + 1) * LANES, :] = jnp.broadcast_to(rounded[:, h * LANES:(h + 1) * LANES], (LANES, LANES)).T

    def rows_of(s):
        first, last = SECTIONS[s]
        return pl.ds(first * QROWS, (last - first) * QROWS)

    def u_copy(par, s, dest, slot):
        here = ubuf.at[par, me, rows_of(s)]
        return pltpu.make_async_remote_copy(src_ref=here, dst_ref=here, send_sem=send_sem.at[par, s, slot], recv_sem=recv_sem.at[par, s, me], device_id={'feat': dest}, device_id_type=MESH)

    def u_send(par, s):
        for slot, d in enumerate(far_order):
            u_copy(par, s, 2 * lax.rem(chip + d, chips) + 1, slot).start()

        @pl.when(core == 0)
        def _():
            u_copy(par, s, sibling, chips - 1).start()

    def u_wait_sends(par):
        for s in range(len(SECTIONS)):
            for slot in range(chips - 1):
                u_copy(par, s, sibling, slot).wait_send()

            @pl.when(core == 0)
            def _():
                u_copy(par, s, sibling, chips - 1).wait_send()

    def u_store(par, b, h, values):
        ubuf[par, me, pl.ds(b * QROWS + h * ROWS, ROWS), :] = values.astype(jnp.bfloat16)

    def first_products(b):
        rhs = []
        for m in range(ROWS):
            rhs.append(jnp.concatenate([xv[pl.ds(b * BLOCK + (h * ROWS + m) * LANES, LANES), :] for h in range(2)], axis=0))
        half = ROWS // 2
        out = []
        for p in range(2):
            left = dmat[:, p * half * TILE:(p + 1) * half * TILE]
            right = jnp.concatenate(rhs[p * half:(p + 1) * half], axis=1)
            out.append(lax.dot_general(left, right, (((1,), (1,)), ((), ())), preferred_element_type=jnp.float32))
        for h in range(2):
            cols = slice(h * LANES, (h + 1) * LANES)
            u_store(0, b, h, jnp.where(row16 < half, out[0][:, cols], out[1][:, cols]))

    def transpose_block(b):
        for m in range(ROWS):
            for h in range(2):
                xt[pl.ds(b * BLOCK + m * TILE, TILE), h * LANES:(h + 1) * LANES] = xv[pl.ds(b * BLOCK + (h * ROWS + m) * LANES, LANES), :].T

    def vector_products(b, h):
        accs = [None] * (ROWS - MATMUL_ROWS)
        for f in range(0, TILE, ROWS):
            d = dcol[f:f + ROWS, :]
            for i in range(len(accs)):
                t = xt[pl.ds(b * BLOCK + (MATMUL_ROWS + i) * TILE + f, ROWS), h * LANES:(h + 1) * LANES].astype(jnp.float32) * d
                t = t[:SUB] + t[SUB:]
                accs[i] = t if accs[i] is None else accs[i] + t
        return [jnp.sum(a, axis=0, keepdims=True) for a in accs]

    def section_products(par, s):
        first, last = SECTIONS[s]
        for b in range(first, last):
            if last - first > 1:
                u = jnp.dot(dmat[:, :MATMUL_ROWS * TILE], xt[pl.ds(b * BLOCK, MATMUL_ROWS * TILE), :], preferred_element_type=jnp.float32)
                parts = [u[:, :LANES], u[:, LANES:]]
            else:
                half = MATMUL_ROWS // 2
                out = [jnp.dot(dmat[:, p * half * TILE:(p + 1) * half * TILE], xt[pl.ds(b * BLOCK + p * half * TILE, half * TILE), :], preferred_element_type=jnp.float32) for p in range(2)]
                parts = [jnp.where(row16 < half, out[0][:, cols], out[1][:, cols]) for cols in (slice(0, LANES), slice(LANES, TILE))]
            for h in range(2):
                high = parts[h][SUB:]
                for i, total in enumerate(vector_products(b, h)):
                    high = jnp.where(row8 == MATMUL_ROWS + i - SUB, total, high)
                u_store(par, b, h, jnp.concatenate([parts[h][:SUB], high], axis=0))

    def products(par):
        for s in range(len(SECTIONS)):
            section_products(par, s)
            u_send(par, s)

    def r_copy(buf, s):
        here = buf.at[rows_of(s)]
        return pltpu.make_async_remote_copy(src_ref=here, dst_ref=here, send_sem=rsend_sem.at[s], recv_sem=rrecv_sem.at[s], device_id={'feat': sibling}, device_id_type=MESH)

    def new_residual(par, s, factor):
        rows = rows_of(s)
        for d in range(1, size):
            src = lax.rem(me + d, size)
            there = ubuf.at[par, src, rows]
            pltpu.make_async_remote_copy(src_ref=there, dst_ref=there, send_sem=send_sem.at[par, s, 0], recv_sem=recv_sem.at[par, s, src], device_id={'feat': src}, device_id_type=MESH).wait_recv()
        total = ubuf[par, 0, rows, :].astype(jnp.float32)
        for k in range(1, size):
            total = total + ubuf[par, k, rows, :].astype(jnp.float32)
        return res[rows, :] - factor * total

    def gradient(par, factor):
        for s in range(len(SECTIONS)):
            first, last = SECTIONS[s]
            rows = rows_of(s)

            @pl.when(lead)
            def _():
                r = new_residual(par, s, factor)
                res[rows, :] = r
                rbf[rows, :] = r.astype(jnp.bfloat16)
                r_copy(rbf, s).start()

            @pl.when(core == 0)
            def _():
                r_copy(rbf, s).wait_recv()

            pieces = []
            for k in range(first * QROWS, last * QROWS):
                r16 = rbf[pl.ds(k // ROWS * ROWS, ROWS), :]
                pieces.append(jnp.where(row16 == k % ROWS, r16.astype(jnp.float32), 0.0).astype(jnp.bfloat16))
            half = len(pieces) // 2
            sums = []
            for q in range(2):
                left = jnp.concatenate(pieces[q * half:(q + 1) * half], axis=1)
                g = jnp.dot(left, xv[pl.ds(first * BLOCK + q * half * LANES, half * LANES), :], preferred_element_type=jnp.float32)
                if s:
                    g = gref[q] + g
                if s < len(SECTIONS) - 1:
                    gref[q] = g
                sums.append(jnp.sum(g, axis=0, keepdims=True))
        return (sums[0] + sums[1]) * (1.0 / samples)

    def update(grad):
        weights = wcur[...]
        eta = eta_v[...]
        threshold = eta * lasso_weight
        stepped = weights + eta * grad
        shrunk = jnp.maximum(stepped - threshold, 0.0) + jnp.minimum(stepped + threshold, 0.0)
        change = shrunk - weights
        wcur[...] = weights + COMBINE_WEIGHT * change
        set_left(change, MATMUL_ROWS)
        set_column(change)

    small[0].wait()
    set_left(wcur[...], ROWS)
    for s, (first, last) in enumerate(SECTIONS):
        for b in range(first, last):
            loads[b].wait()
            first_products(b)
            transpose_block(b)
        if s == 0:
            pl.semaphore_wait(barrier, size - 1)
        u_send(0, s)
    small[1].wait()
    small[2].wait()

    @pl.loop(0, SWEEPS)
    def _(t):
        par = lax.rem(t, 2)
        factor = jnp.where(t == 0, 1.0, COMBINE_WEIGHT).astype(jnp.float32)
        update(gradient(par, factor))
        products(1 - par)
        u_wait_sends(par)

        @pl.when(lead)
        def _():
            for s in range(len(SECTIONS)):
                r_copy(rbf, s).wait_send()

    par = SWEEPS % 2
    w_out[...] = wcur[...]
    for s in range(len(SECTIONS)):
        @pl.when(lead)
        def _():
            res[rows_of(s), :] = new_residual(par, s, COMBINE_WEIGHT)
            r_copy(res, s).start()
    for s in range(len(SECTIONS)):
        @pl.when(core == 0)
        def _():
            r_copy(res, s).wait_recv()
    r_out[...] = res[...]
    u_wait_sends(par)

    @pl.when(lead)
    def _():
        for s in range(len(SECTIONS)):
            r_copy(res, s).wait_send()


def solution(mesh):
    size = mesh.shape['feat']

    def local_run(x_local, coef_local, targets_local, step_local):
        samples, feats = x_local.shape
        sections = len(SECTIONS)
        lasso_weight = 0.3 * size / (feats * size) ** 0.5
        vmem = pl.BlockSpec(memory_space=pltpu.VMEM)
        anywhere = pl.BlockSpec(memory_space=pl.ANY)
        weights, residual = pl.pallas_call(
            functools.partial(kernel, size, lasso_weight),
            out_shape=(jax.ShapeDtypeStruct((1, feats), jnp.float32), jax.ShapeDtypeStruct((samples // LANES, LANES), jnp.float32)),
            in_specs=[anywhere] * 4,
            out_specs=(vmem, vmem),
            scratch_shapes=[
                pltpu.VMEM((samples, feats), jnp.bfloat16),
                pltpu.VMEM((samples, feats), jnp.bfloat16),
                pltpu.VMEM((2, size, samples // LANES, LANES), jnp.bfloat16),
                pltpu.VMEM((samples // LANES, LANES), jnp.bfloat16),
                pltpu.VMEM((samples // LANES, LANES), jnp.float32),
                pltpu.VMEM((ROWS, ROWS * feats), jnp.bfloat16),
                pltpu.VMEM((feats, LANES), jnp.float32),
                pltpu.VMEM((2, ROWS, feats), jnp.float32),
                pltpu.VMEM((1, feats), jnp.float32),
                pltpu.VMEM((1, feats), jnp.float32),
                pltpu.SemaphoreType.DMA((samples // BLOCK,)),
                pltpu.SemaphoreType.DMA((3,)),
                pltpu.SemaphoreType.DMA((2, sections, size // 2)),
                pltpu.SemaphoreType.DMA((2, sections, size)),
                pltpu.SemaphoreType.DMA((sections,)),
                pltpu.SemaphoreType.DMA((sections,)),
            ],
            compiler_params=pltpu.CompilerParams(collective_id=0, has_side_effects=True),
        )(x_local, coef_local.reshape(1, feats), targets_local.reshape(samples // LANES, LANES), step_local.reshape(1, feats))
        return weights.reshape(feats, 1), residual.reshape(samples, 1)

    return jax.shard_map(local_run, mesh=mesh, in_specs=(P('prob', 'feat'), P(('prob', 'feat'), None), P('prob', None), P(('prob', 'feat'))), out_specs=(P(('prob', 'feat'), None), P('prob', None)), check_vma=False)
```

time: 463 us -> 52.2 us (0.11)
  waiting for transfers between devices: 369 us -> 0 us
  matrix products: 67.1 us -> 0 us
  Pallas kernels: 0 us -> 48.7 us
  between operations: 14.2 us -> 0.64 us
  other arithmetic: 9.7 us -> 0 us
    psum x7 -> x0, waiting for transfers between devices: 369 us -> none  [summed_product(): return lax.psum(product.astype(jnp.bfloat16).astype(jnp.float32), 'feat')]
    dot_general x13 -> x0, matrix products: 67.1 us -> none  [the longest x7 39.5 us: summed_product(): jnp.dot(x_local, values.astype(jnp.bfloat16), preferred_element_type=jnp....]
    pallas_call x0 -> x1, Pallas kernels: none -> 48.7 us  [local_run(): pl.pallas_call(functools.partial(kernel, size, lasso_weight), out_shape=(...]
  transfers between devices with their start and end apart: 7 -> 0, of which waited for: 7 -> 0; matrix products, arithmetic and copies ran while one was open for 0% -> 0% of each run, Pallas kernels for 0% -> 0%
where the time goes in v3:
time: 52.2 us; the launch traced here: 52 us
  Pallas kernels  48.7 us (93%)
  local copies, waits for them, and re-layouts  2.67 us (5%)
  between operations  0.64 us (1%)
    pallas_call x1, Pallas kernels, local_run(): pl.pallas_call(functools.partial(kernel, size, lasso_weight), out_shape=(...  48.7 us
    unnamed x2, local copies, waits for them, and re-layouts  2.67 us

profile of v3, /device:TPU:81, one launch (start us, length us, event | category | flops | bytes accessed | tf_op | source)
XLA Modules:
  0.0 52.0 jit_solution(13582068551585520522)
XLA Ops:
  0.6 48.7 %shard_map.59 = (f32[1,256]{1,0:T(1,128)}, f32[128,128]{1,0:T(8,128)}) custom-call(bf16[16384,256]{1,0:T(8,128)(2,1)} %x_hbm.1, f32[1,256]{1,0:T(1,128)} %bitcast.7, f32[128,128]{1,0:T(8,128)} %bitcast.5, f32[1,256]{1,0:T(1,128)} %bitcast.8), custom_call_target="tpu_custom_call" | custom-call | tf_op jit(solution)/shard_map/pallas_call | solution.py:250
  49.3 1.2 %copy.8 = f32[256,1]{0,1:T(1,128)} copy(f32[256,1]{0,1:T(1,128)} %bitcast.9) | data formatting | bytes 2048
  50.5 1.5 %copy.9 = f32[16384,1]{0,1:T(1,128)} copy(f32[16384,1]{0,1:T(1,128)} %bitcast.6) | data formatting | bytes 131072

commit v4 on v3

--- a/solution.py
+++ b/solution.py
@@ -17,6 +17,7 @@
 BLOCK = ROWS * TILE
 QROWS = BLOCK // LANES
 MATMUL_ROWS = 10
+FENCE = 4
 SECTIONS = ((0, 2), (2, 4))
 
 
@@ -103,31 +104,43 @@
             for h in range(2):
                 xt[pl.ds(b * BLOCK + m * TILE, TILE), h * LANES:(h + 1) * LANES] = xv[pl.ds(b * BLOCK + (h * ROWS + m) * LANES, LANES), :].T
 
-    def vector_products(b, h):
-        accs = [None] * (ROWS - MATMUL_ROWS)
-        for f in range(0, TILE, ROWS):
-            d = dcol[f:f + ROWS, :]
-            for i in range(len(accs)):
-                t = xt[pl.ds(b * BLOCK + (MATMUL_ROWS + i) * TILE + f, ROWS), h * LANES:(h + 1) * LANES].astype(jnp.float32) * d
-                t = t[:SUB] + t[SUB:]
-                accs[i] = t if accs[i] is None else accs[i] + t
-        return [jnp.sum(a, axis=0, keepdims=True) for a in accs]
-
     def section_products(par, s):
         first, last = SECTIONS[s]
-        for b in range(first, last):
+        if last - first > 1:
+            chains = [(b, range(MATMUL_ROWS)) for b in range(first, last)]
+        else:
+            chains = [(first, range(p * MATMUL_ROWS // 2, (p + 1) * MATMUL_ROWS // 2)) for p in range(2)]
+        groups = [(b, h) for b in range(first, last) for h in range(2)]
+        spare = ROWS - MATMUL_ROWS
+        accs = {}
+
+        def vector_step(b, h, f, i):
+            t = xt[pl.ds(b * BLOCK + (MATMUL_ROWS + i) * TILE + f, ROWS), h * LANES:(h + 1) * LANES].astype(jnp.float32) * dcol[f:f + ROWS, :]
+            t = t[:SUB] + t[SUB:]
+            accs[b, h, i] = accs[b, h, i] + t if f else t
+
+        pending = [(b, h, f, i) for b, h in groups for f in range(0, TILE, ROWS) for i in range(spare)]
+        steps = len(chains[0][1])
+        outs = [None] * len(chains)
+        for k in range(steps):
+            for c, (b, ms) in enumerate(chains):
+                m = ms[k]
+                u = jnp.dot(dmat[:, m * TILE:(m + 1) * TILE], xt[pl.ds(b * BLOCK + m * TILE, TILE), :], preferred_element_type=jnp.float32)
+                outs[c] = u if k == 0 else outs[c] + u
+            for args in pending[len(pending) * k // steps:len(pending) * (k + 1) // steps]:
+                vector_step(*args)
+            if k + 1 < steps and (k + 1) % FENCE == 0:
+                pl.delay(1)
+        for b, h in groups:
+            cols = slice(h * LANES, (h + 1) * LANES)
             if last - first > 1:
-                u = jnp.dot(dmat[:, :MATMUL_ROWS * TILE], xt[pl.ds(b * BLOCK, MATMUL_ROWS * TILE), :], preferred_element_type=jnp.float32)
-                parts = [u[:, :LANES], u[:, LANES:]]
+                u = outs[b - first][:, cols]
             else:
-                half = MATMUL_ROWS // 2
-                out = [jnp.dot(dmat[:, p * half * TILE:(p + 1) * half * TILE], xt[pl.ds(b * BLOCK + p * half * TILE, half * TILE), :], preferred_element_type=jnp.float32) for p in range(2)]
-                parts = [jnp.where(row16 < half, out[0][:, cols], out[1][:, cols]) for cols in (slice(0, LANES), slice(LANES, TILE))]
-            for h in range(2):
-                high = parts[h][SUB:]
-                for i, total in enumerate(vector_products(b, h)):
-                    high = jnp.where(row8 == MATMUL_ROWS + i - SUB, total, high)
-                u_store(par, b, h, jnp.concatenate([parts[h][:SUB], high], axis=0))
+                u = jnp.where(row16 < MATMUL_ROWS // 2, outs[0][:, cols], outs[1][:, cols])
+            high = u[SUB:]
+            for i in range(spare):
+                high = jnp.where(row8 == MATMUL_ROWS + i - SUB, jnp.sum(accs[b, h, i], axis=0, keepdims=True), high)
+            u_store(par, b, h, jnp.concatenate([u[:SUB], high], axis=0))
 
     def products(par):
         for s in range(len(SECTIONS)):
@@ -165,20 +178,21 @@
             def _():
                 r_copy(rbf, s).wait_recv()
 
-            pieces = []
-            for k in range(first * QROWS, last * QROWS):
-                r16 = rbf[pl.ds(k // ROWS * ROWS, ROWS), :]
-                pieces.append(jnp.where(row16 == k % ROWS, r16.astype(jnp.float32), 0.0).astype(jnp.bfloat16))
-            half = len(pieces) // 2
-            sums = []
+            pieces = (last - first) * ROWS
+            sums = [None] * 2
+            for j in range(pieces // 2):
+                for q in range(2):
+                    k = first * QROWS + q * pieces + 2 * j
+                    r16 = rbf[pl.ds(k // ROWS * ROWS, ROWS), :].astype(jnp.float32)
+                    left = jnp.concatenate([jnp.where(row16 == (k + e) % ROWS, r16, 0.0).astype(jnp.bfloat16) for e in range(2)], axis=1)
+                    g = jnp.dot(left, xv[pl.ds(k * LANES, TILE), :], preferred_element_type=jnp.float32)
+                    sums[q] = g if j == 0 else sums[q] + g
             for q in range(2):
-                left = jnp.concatenate(pieces[q * half:(q + 1) * half], axis=1)
-                g = jnp.dot(left, xv[pl.ds(first * BLOCK + q * half * LANES, half * LANES), :], preferred_element_type=jnp.float32)
                 if s:
-                    g = gref[q] + g
+                    sums[q] = gref[q] + sums[q]
                 if s < len(SECTIONS) - 1:
-                    gref[q] = g
-                sums.append(jnp.sum(g, axis=0, keepdims=True))
+                    gref[q] = sums[q]
+        sums = [jnp.sum(g, axis=0, keepdims=True) for g in sums]
         return (sums[0] + sums[1]) * (1.0 / samples)
 
     def update(grad):

time: 52.2 us -> 50.6 us (0.969)
  Pallas kernels: 48.7 us -> 47.1 us
    pallas_call x1, Pallas kernels: 48.7 us -> 47.1 us  [local_run(): pl.pallas_call(functools.partial(kernel, size, lasso_weight), out_shape=(...]
where the time goes in v4:
time: 50.6 us; the launch traced here: 50.5 us
  Pallas kernels  47.1 us (93%)
  local copies, waits for them, and re-layouts  2.67 us (5%)
  between operations  0.64 us (1%)
    pallas_call x1, Pallas kernels, local_run(): pl.pallas_call(functools.partial(kernel, size, lasso_weight), out_shape=(...  47.1 us
    unnamed x2, local copies, waits for them, and re-layouts  2.67 us

profile of v4, /device:TPU:81, one launch (start us, length us, event | category | flops | bytes accessed | tf_op | source)
XLA Modules:
  0.0 50.5 jit_solution(3283012634915952559)
XLA Ops:
  0.6 47.1 %shard_map.59 = (f32[1,256]{1,0:T(1,128)}, f32[128,128]{1,0:T(8,128)}) custom-call(bf16[16384,256]{1,0:T(8,128)(2,1)} %x_hbm.1, f32[1,256]{1,0:T(1,128)} %bitcast.7, f32[128,128]{1,0:T(8,128)} %bitcast.5, f32[1,256]{1,0:T(1,128)} %bitcast.8), custom_call_target="tpu_custom_call" | custom-call | tf_op jit(solution)/shard_map/pallas_call | solution.py:264
  47.8 1.2 %copy.8 = f32[256,1]{0,1:T(1,128)} copy(f32[256,1]{0,1:T(1,128)} %bitcast.9) | data formatting | bytes 2048
  49.0 1.5 %copy.9 = f32[16384,1]{0,1:T(1,128)} copy(f32[16384,1]{0,1:T(1,128)} %bitcast.6) | data formatting | bytes 131072

commit v5 on v4

--- a/solution.py
+++ b/solution.py
@@ -263,7 +263,7 @@
         anywhere = pl.BlockSpec(memory_space=pl.ANY)
         weights, residual = pl.pallas_call(
             functools.partial(kernel, size, lasso_weight),
-            out_shape=(jax.ShapeDtypeStruct((1, feats), jnp.float32), jax.ShapeDtypeStruct((samples // LANES, LANES), jnp.float32)),
+            out_shape=(pltpu.VMEM((1, feats), jnp.float32), pltpu.VMEM((samples // LANES, LANES), jnp.float32)),
             in_specs=[anywhere] * 4,
             out_specs=(vmem, vmem),
             scratch_shapes=[

time: 50.6 us -> 48.4 us (0.957)
  local copies, waits for them, and re-layouts: 2.67 us -> 1.19 us
  Pallas kernels: 47.1 us -> 46.5 us
    unnamed x2, local copies, waits for them, and re-layouts: 2.67 us -> 1.19 us
    pallas_call x1, Pallas kernels: 47.1 us -> 46.5 us  [local_run(): pl.pallas_call(functools.partial(kernel, size, lasso_weight), out_shape=(...]
where the time goes in v5:
time: 48.4 us; the launch traced here: 48.3 us
  Pallas kernels  46.5 us (96%)
  local copies, waits for them, and re-layouts  1.19 us (2%)
  between operations  0.64 us (1%)
    pallas_call x1, Pallas kernels, local_run(): pl.pallas_call(functools.partial(kernel, size, lasso_weight), out_shape=(...  46.5 us
    unnamed x2, local copies, waits for them, and re-layouts  1.19 us

profile of v5, /device:TPU:81, one launch (start us, length us, event | category | flops | bytes accessed | tf_op | source)
XLA Modules:
  0.0 48.3 jit_solution(6048410167234967004)
XLA Ops:
  0.6 46.5 %shard_map.59 = (f32[1,256]{1,0:T(1,128)S(1)}, f32[128,128]{1,0:T(8,128)S(1)}) custom-call(bf16[16384,256]{1,0:T(8,128)(2,1)} %x_hbm.1, f32[1,256]{1,0:T(1,128)} %bitcast.8, f32[128,128]{1,0:T(8,128)} %bitcast.7, f32[1,256]{1,0:T(1,128)} %bitcast.9), custom_call_target="tpu_custom_call" | custom-call | tf_op jit(solution)/shard_map/pallas_call | solution.py:264
  47.1 0.6 %copy.8 = f32[256,1]{0,1:T(1,128)} copy(f32[256,1]{0,1:T(1,128)S(1)} %bitcast.6) | data formatting | bytes 2048
  47.7 0.6 %copy.9 = f32[16384,1]{0,1:T(1,128)} copy(f32[16384,1]{0,1:T(1,128)S(1)} %bitcast.5) | data formatting | bytes 131072
